TPU v7x, 512 devices: a whole 4x8x8 slice. The times are simulated.
512 devices in a mesh: level: 2 (over z_lo), row: 16 (over y, core), col: 16 (over x, z_hi).
Axes of the slice: x: 4, y: 8, z: 8 (z_hi: 4, z_lo: 2; z = z_hi * 2 + z_lo), core: 2. Of those that a mesh axis runs over, the one named last changes fastest.
Arguments:
- initial: float32 [3, 2048, 16384], P(None, 'row', 'col'), may hold values from -0.75 to 0.75
Outputs:
- levels_out: float32 [2, 3, 2048, 16384], P('level', None, 'row', 'col')
All inputs are finite; a program needn't handle non-finite values.
Results may differ from a plain program's by a relative error of at most 0.00002.
Values sent between devices are 32-bit elements; how exact they have to be, the bound alone decides.
A program may use at most 64 MiB of HBM per device.

v0:
```python
import functools

import jax
import jax.numpy as jnp
from jax import lax
from jax.experimental import pallas as pl
from jax.experimental.pallas import tpu as pltpu
from jax.sharding import PartitionSpec as P

STEPS = 8
TIME_STEP = 0.1
GRAVITY = 1.0
ROTATION = 0.2

HALF = 0.5 * TIME_STEP
SCALES = (HALF * HALF * GRAVITY, HALF, HALF)
REST = HALF * HALF * GRAVITY
TURN = TIME_STEP * ROTATION

ROWS = 128
COLS = 1024
TILES = COLS // 128
STRIP = 9
STRIPS = 16
PITCH = 11
FRONT = 16
SPAN = 128 + 2 * FRONT
WORDS = SPAN * PITCH
VMEM = pltpu.VMEM


def exchange_kernel(rows_n, cols_n, x, north, south, sides, corners,
                    top, bottom, left, right, packed, corner_out, local, send, recv):
    me_r, me_c = lax.axis_index("row"), lax.axis_index("col")
    up, down = lax.rem(me_r + rows_n - 1, rows_n), lax.rem(me_r + 1, rows_n)
    west, east = lax.rem(me_c + cols_n - 1, cols_n), lax.rem(me_c + 1, cols_n)
    places = [(up, me_c), (down, me_c), (me_r, west), (me_r, east), (up, west), (up, east), (down, west), (down, east)]
    ids = [{"row": r, "col": c} for r, c in places]
    barrier = pltpu.get_barrier_semaphore()
    for where in ids:
        pl.semaphore_signal(barrier, inc=1, device_id=where, device_id_type=pl.DeviceIdType.MESH)
    loads = [
        pltpu.make_async_copy(x.at[:, :, 0:128], left, local.at[0]),
        pltpu.make_async_copy(x.at[:, :, COLS - 128:COLS], right, local.at[1]),
        pltpu.make_async_copy(x.at[:, 0:16, :], top, local.at[2]),
        pltpu.make_async_copy(x.at[:, ROWS - 16:ROWS, :], bottom, local.at[3]),
    ]
    for load in loads:
        load.start()
    loads[0].wait()
    loads[1].wait()
    lane = lax.broadcasted_iota(jnp.int32, (16, 128), 1)
    for f in range(3):
        packed[0, f] = jnp.transpose(left[f])[0:16]
        packed[1, f] = jnp.transpose(right[f])[112:128]
    for k, (ref, row0, lane0) in enumerate(((left, 0, 0), (right, 0, 112), (left, ROWS - 16, 0), (right, ROWS - 16, 112))):
        out = ref[0, row0:row0 + 16]
        if lane0:
            out = pltpu.roll(out, 128 - lane0, 1)
        for f in (1, 2):
            piece = pltpu.roll(ref[f, row0:row0 + 16], (128 - lane0 + 16 * f) % 128, 1)
            out = jnp.where(lane < 16 * f, out, piece)
        corner_out[k] = out
    loads[2].wait()
    loads[3].wait()
    pl.semaphore_wait(barrier, 8)
    sends = []
    pieces = [
        (top, south), (bottom, north),
        (packed.at[0], sides.at[0]), (packed.at[1], sides.at[1]),
        (corner_out.at[0], corners.at[3]), (corner_out.at[1], corners.at[2]),
        (corner_out.at[2], corners.at[1]), (corner_out.at[3], corners.at[0]),
    ]
    for k, (src, dst) in enumerate(pieces):
        sends.append(pltpu.make_async_remote_copy(
            src_ref=src, dst_ref=dst, send_sem=send.at[k], recv_sem=recv.at[k],
            device_id=ids[k], device_id_type=pl.DeviceIdType.MESH))
    for k in (4, 5, 6, 7, 2, 3, 0, 1):
        sends[k].start()
    for one in sends:
        one.wait()


def exchange(x, rows_n, cols_n):
    f32 = jnp.float32
    any_spec = pl.BlockSpec(memory_space=pl.ANY)
    return pl.pallas_call(
        functools.partial(exchange_kernel, rows_n, cols_n),
        out_shape=(
            jax.ShapeDtypeStruct((3, 16, COLS), f32),
            jax.ShapeDtypeStruct((3, 16, COLS), f32),
            jax.ShapeDtypeStruct((2, 3, 16, 128), f32),
            jax.ShapeDtypeStruct((4, 16, 128), f32),
        ),
        in_specs=[any_spec],
        out_specs=(any_spec,) * 4,
        scratch_shapes=[
            VMEM((3, 16, COLS), f32),
            VMEM((3, 16, COLS), f32),
            VMEM((3, ROWS, 128), f32),
            VMEM((3, ROWS, 128), f32),
            VMEM((2, 3, 16, 128), f32),
            VMEM((4, 16, 128), f32),
            pltpu.SemaphoreType.DMA((4,)),
            pltpu.SemaphoreType.DMA((8,)),
            pltpu.SemaphoreType.DMA((8,)),
        ],
        compiler_params=pltpu.CompilerParams(collective_id=0, has_side_effects=True),
    )(x)


def word(q, r):
    return (q + FRONT) * PITCH + r + 1


def take(ref, q, r):
    return ref[pl.ds(word(q, r), 8, stride=PITCH), :]


def put(ref, q, r, value):
    ref[pl.ds(word(q, r), 8, stride=PITCH), :] = value


def slopes(state, q0, act):
    e_ref, u_ref, v_ref, w_ref = state

    def load(r):
        e, u, v = take(e_ref, q0, r), take(u_ref, q0, r), take(v_ref, q0, r)
        return e, u, v, (e + REST) * u

    below, here = load(-1), load(0)
    for r in range(STRIP):
        above = load(r + 1)
        e, u, v, _ = here
        de, du, dv, dw = (a - b for a, b in zip(above, below))
        ye = take(e_ref, q0 + 1, r) - take(e_ref, q0 - 1, r)
        yu = take(u_ref, q0 + 1, r) - take(u_ref, q0 - 1, r)
        yv = take(v_ref, q0 + 1, r) - take(v_ref, q0 - 1, r)
        yw = take(w_ref, q0 + 1, r) - take(w_ref, q0 - 1, r)
        ge = dw + yw
        gu = (u * du + v * (yu - TURN)) + de
        gv = (u * (dv + TURN) + v * yv) + ye
        act(r, (e, u, v), (ge, gu, gv))
        below, here = here, above


def edges(refs, q0):
    for ref in refs:
        put(ref, q0, -1, pltpu.roll(take(ref, q0, STRIP - 1), TILES, 1))
        put(ref, q0, STRIP, pltpu.roll(take(ref, q0, 0), 128 - TILES, 1))


def sweep(first, blocks, work, late, unroll):
    trips, rest = divmod(blocks, unroll)

    def trip(start, count, before):
        for k in range(count):
            work(start + 8 * k)
        for k in range(before):
            late(start + 8 * (k - before))

    trip(first, unroll, 0)

    def step(i, carry):
        trip(first + 8 * unroll * i, unroll, unroll)
        return carry

    lax.fori_loop(1, trips, step, 0)
    last = first + 8 * unroll * trips
    if rest:
        trip(last, rest, unroll)
        left = [last + 8 * k for k in range(rest)]
    else:
        left = [last + 8 * (k - unroll) for k in range(unroll)]

    def finish():
        for q in left:
            late(q)

    return finish


def window_kernel(x, north, south, sides, corners, out,
                  grid, turned, side_in, corner_in, pe, pu, pv, pw, qe, qu, qv, qw,
                  ce, cu, cv, cw, de, du, dv, sems, out_sems):
    level = lax.axis_index("level")
    copies = []

    def fetch(src, dst):
        copies.append(pltpu.make_async_copy(src, dst, sems.at[len(copies)]))
        copies[-1].start()

    view = x.reshape(3, 16, 8, COLS)
    n_view, s_view = north.reshape(3, 2, 8, COLS), south.reshape(3, 2, 8, COLS)
    for c in range(TILES):
        cut = slice(128 * c, 128 * c + 128)
        fetch(view.at[:, :, :, cut], grid.at[:, 2:18, c + 1])
        fetch(n_view.at[:, :, :, cut], grid.at[:, 0:2, c + 1])
        fetch(s_view.at[:, :, :, cut], grid.at[:, 18:20, c + 1])
    fetch(sides.at[0], side_in.at[:, 0:16])
    fetch(sides.at[1], side_in.at[:, 112:128])
    fetch(corners, corner_in)
    for copy in copies:
        copy.wait()

    lane8 = lax.broadcasted_iota(jnp.int32, (8, 128), 1)
    for f in range(3):
        beside = jnp.transpose(side_in[f])
        for t in range(16):
            part = beside[8 * t:8 * t + 8]
            grid[f, t + 2, 0] = part
            grid[f, t + 2, TILES + 1] = part
        for t in range(2):
            for k, place in ((0, 0), (2, 18)):
                west = corner_in[k, 8 * t:8 * t + 8]
                east = corner_in[k + 1, 8 * t:8 * t + 8]
                west = pltpu.roll(west, (112 - 16 * f) % 128, 1)
                if f:
                    east = pltpu.roll(east, 128 - 16 * f, 1)
                grid[f, place + t, 0] = west
                grid[f, place + t, TILES + 1] = east

    flat = grid.reshape(3, 20 * 10 * 8, 128)

    def tile_row(f, i, shift):
        i = i + 16
        return flat[f, pl.ds((i // 8) * 80 + 8 * (1 + shift) + i % 8, TILES, stride=8), :]

    for r in range(-1, STRIP + 1):
        for f, ref in enumerate((pe, pu, pv)):
            here, beside = [], []
            for s in range(STRIPS):
                i = s * STRIP + r - 8
                here.append(tile_row(f, i, 0))
                beside.append(jnp.where(lane8 >= 64, tile_row(f, i, -1), tile_row(f, i, 1)))
            here = jnp.transpose(jnp.concatenate(here, axis=0)) * SCALES[f]
            beside = jnp.transpose(jnp.concatenate(beside, axis=0)) * SCALES[f]
            for k in range(16):
                put(ref, 8 * k, r, here[8 * k:8 * k + 8])
            put(ref, -16, r, beside[112:120])
            put(ref, -8, r, beside[120:128])
            put(ref, 128, r, beside[0:8])
            put(ref, 136, r, beside[8:16])

    def weigh(i, carry):
        at = pl.ds(pl.multiple_of(i * 8 * 11, 8), 8 * 11)
        pw[at, :] = (pe[at, :] + REST) * pv[at, :]
        return carry

    lax.fori_loop(0, SPAN // 8, weigh, 0)

    def keep(refs, q, r, values):
        for ref, value in zip(refs, values):
            put(ref, q, r, value)

    def weighed(values):
        e, u, v = values
        return e, u, v, (e + REST) * v

    a_state, b_state = (pe, pu, pv, pw), (qe, qu, qv, qw)
    c_state, d_state = (ce, cu, cv, cw), (de, du, dv)
    nothing = lambda q: None

    def predict(now, then, m, with_c):
        def work(q0):
            def act(r, own, change):
                new = tuple(p - g for p, g in zip(own, change))
                keep(then, q0, r, weighed(new))
                if with_c and m == 0:
                    keep(d_state, q0, r, tuple(p - 0.5 * g for p, g in zip(own, change)))
                elif with_c:
                    mid = tuple(take(ref, q0, r) - 0.5 * g for ref, g in zip(d_state, change))
                    keep(c_state, q0, r, weighed(mid))

            slopes(now, q0, act)

        def late(q0):
            if with_c and m:
                edges(c_state[:3], q0)
            edges(then[:3], q0)

        reach = STEPS - m
        return sweep(-reach, (128 + 2 * reach + 7) // 8, work, late, 2)

    def correct(m):
        def work(q0):
            def act(r, own, change):
                keep(d_state, q0, r, tuple(take(ref, q0, r) - g for ref, g in zip(d_state, change)))

            slopes(c_state, q0, act)

        reach = STEPS - 1 - m
        return sweep(-reach, (128 + 2 * reach + 7) // 8, work, nothing, 2)

    def last():
        def work(q0):
            def act(r, own, change):
                keep(c_state, q0, r, tuple(take(ref, q0, r) - 0.5 * g for ref, g in zip(d_state, change)))

            slopes(a_state, q0, act)

        sweep(0, 16, work, nothing, 2)

    def emit(refs):
        done = []
        for f, ref in enumerate(refs):
            for r in range(STRIP):
                block = jnp.concatenate([take(ref, 8 * k, r) for k in range(16)], axis=0)
                block = jnp.transpose(block) * (1.0 / SCALES[f])
                for s in range(STRIPS):
                    i = s * STRIP + r - 8
                    if 0 <= i < ROWS:
                        flat[f, pl.ds((i // 8) * 80 + 8 + i % 8, TILES, stride=8), :] = block[8 * s:8 * s + 8]
            target = out.reshape(1, 3, 16, 8, COLS)
            for c in range(TILES):
                copy = pltpu.make_async_copy(
                    grid.at[f, 0:16, c + 1], target.at[0, f, :, :, 128 * c:128 * c + 128], out_sems.at[f * TILES + c])
                copy.start()
                done.append(copy)
        for copy in done:
            copy.wait()

    @pl.when(level == 0)
    def _():
        for m in range(STEPS):
            now, then = (a_state, b_state) if m % 2 == 0 else (b_state, a_state)
            predict(now, then, m, False)()
        emit(a_state[:3])

    @pl.when(level == 1)
    def _():
        for m in range(STEPS):
            now, then = (a_state, b_state) if m % 2 == 0 else (b_state, a_state)
            predict(now, then, m, True)()
            if m:
                correct(m)
        last()
        emit(c_state[:3])


def window(x, north, south, sides, corners):
    f32 = jnp.float32
    any_spec = pl.BlockSpec(memory_space=pl.ANY)
    return pl.pallas_call(
        window_kernel,
        out_shape=jax.ShapeDtypeStruct((1, 3, ROWS, COLS), f32),
        in_specs=[any_spec] * 5,
        out_specs=any_spec,
        scratch_shapes=[
            VMEM((3, 20, 10, 8, 128), f32),
            VMEM((8, 128), f32),
            VMEM((3, 128, 128), f32),
            VMEM((4, 16, 128), f32),
        ] + [VMEM((WORDS, 128), f32) for _ in range(15)] + [
            pltpu.SemaphoreType.DMA((3 * TILES + 3,)),
            pltpu.SemaphoreType.DMA((3 * TILES,)),
        ],
        compiler_params=pltpu.CompilerParams(vmem_limit_bytes=48 * 1024 * 1024),
    )(x, north, south, sides, corners)


def solution(mesh):
    rows_n, cols_n = mesh.shape["row"], mesh.shape["col"]

    def body(x):
        return window(x, *exchange(x, rows_n, cols_n))

    return jax.shard_map(
        body,
        mesh=mesh,
        in_specs=(P(None, "row", "col"),),
        out_specs=P("level", None, "row", "col"),
        check_vma=False,
    )
```

profile of v0, /device:TPU:64, one launch (start us, length us, event | category | flops | bytes accessed | tf_op | source)
XLA Modules:
  0.0 44.5 jit_solution(1724578644023113219)
XLA Ops:
  0.0 0.0 copy-start
  0.0 18.2 %shard_map.17 = (f32[3,16,1024]{2,1,0:T(8,128)}, f32[3,16,1024]{2,1,0:T(8,128)}, f32[2,3,16,128]{3,2,1,0:T(8,128)}, f32[4,16,128]{2,1,0:T(8,128)}) custom-call(f32[3,128,1024]{2,1,0:T(8,128)} %x.3), custom_call_target="tpu_custom_call" | custom-call | tf_op jit(solution)/shard_map/pallas_call | solution.py:87
  18.2 0.0 copy-done
  18.3 0.0 copy-start.1
  18.3 0.9 %copy-done.1 = f32[3,16,1024]{2,1,0:T(8,128)S(1)} copy-done((f32[3,16,1024]{2,1,0:T(8,128)S(1)}, f32[3,16,1024]{2,1,0:T(8,128)}, u32[]{:S(2)}) %copy-start.1) | copy-done | bytes 196632
  19.2 0.0 copy-start.2
  19.2 0.9 %copy-done.2 = f32[3,16,1024]{2,1,0:T(8,128)S(1)} copy-done((f32[3,16,1024]{2,1,0:T(8,128)S(1)}, f32[3,16,1024]{2,1,0:T(8,128)}, u32[]{:S(2)}) %copy-start.2) | copy-done | bytes 196632
  20.1 0.0 copy-start.3
  20.1 0.8 %copy-done.3 = f32[2,3,16,128]{3,2,1,0:T(8,128)S(1)} copy-done((f32[2,3,16,128]{3,2,1,0:T(8,128)S(1)}, f32[2,3,16,128]{3,2,1,0:T(8,128)}, u32[]{:S(2)}) %copy-start.3) | copy-done | bytes 49176
  20.9 0.0 copy-start.4
  20.9 0.8 %copy-done.4 = f32[4,16,128]{2,1,0:T(8,128)S(1)} copy-done((f32[4,16,128]{2,1,0:T(8,128)S(1)}, f32[4,16,128]{2,1,0:T(8,128)}, u32[]{:S(2)}) %copy-start.4) | copy-done | bytes 32792
  21.7 22.8 %shard_map.18 = f32[1,3,128,1024]{3,2,1,0:T(8,128)} custom-call(f32[3,128,1024]{2,1,0:T(8,128)S(1)} %copy-done, f32[3,16,1024]{2,1,0:T(8,128)S(1)} %copy-done.1, f32[3,16,1024]{2,1,0:T(8,128)S(1)} %copy-done.2, f32[2,3,16,128]{3,2,1,0:T(8,128)S(1)} %copy-done.3, f32[4,16,128]{2,1,0:T(8,128)S(1)} %copy-done.4), custom_call_target="tpu_custom_call" | custom-call | tf_op jit(solution)/shard_map/pallas_call | solution.py:344
Async XLA Ops:
  0.0 18.2 %copy-start = (f32[3,128,1024]{2,1,0:T(8,128)S(1)}, f32[3,128,1024]{2,1,0:T(8,128)}, u32[]{:S(2)}) copy-start(f32[3,128,1024]{2,1,0:T(8,128)} %x.3) | copy-start | bytes 4718596
  18.3 0.9 %copy-start.1 = (f32[3,16,1024]{2,1,0:T(8,128)S(1)}, f32[3,16,1024]{2,1,0:T(8,128)}, u32[]{:S(2)}) copy-start(f32[3,16,1024]{2,1,0:T(8,128)} %get-tuple-element.9.north) | copy-start | bytes 589828
  19.2 0.9 %copy-start.2 = (f32[3,16,1024]{2,1,0:T(8,128)S(1)}, f32[3,16,1024]{2,1,0:T(8,128)}, u32[]{:S(2)}) copy-start(f32[3,16,1024]{2,1,0:T(8,128)} %get-tuple-element.10.south) | copy-start | bytes 589828
  20.1 0.8 %copy-start.3 = (f32[2,3,16,128]{3,2,1,0:T(8,128)S(1)}, f32[2,3,16,128]{3,2,1,0:T(8,128)}, u32[]{:S(2)}) copy-start(f32[2,3,16,128]{3,2,1,0:T(8,128)} %get-tuple-element.11.sides) | copy-start | bytes 147460
  20.9 0.8 %copy-start.4 = (f32[4,16,128]{2,1,0:T(8,128)S(1)}, f32[4,16,128]{2,1,0:T(8,128)}, u32[]{:S(2)}) copy-start(f32[4,16,128]{2,1,0:T(8,128)} %get-tuple-element.12.corners) | copy-start | bytes 98308
where the time goes:
time: 44.8 us; the launch traced here: 44.5 us
  Pallas kernels  41.1 us (92%)
  local copies, waits for them, and re-layouts  3.41 us (8%)
    pallas_call x1, Pallas kernels, window(): pl.pallas_call(window_kernel, out_shape=jax.ShapeDtypeStruct((1, 3, ROWS,...  22.8 us
    pallas_call x1, Pallas kernels, exchange(): pl.pallas_call(functools.partial(exchange_kernel, rows_n, cols_n), out_sh...  18.2 us
    unnamed x10, local copies, waits for them, and re-layouts  3.41 us

commit v1 on v0

--- a/solution.py
+++ b/solution.py
@@ -22,7 +22,8 @@
 TILES = COLS // 128
 STRIP = 9
 STRIPS = 16
-PITCH = 11
+PITCH = 9
+RIM = 3
 FRONT = 16
 SPAN = 128 + 2 * FRONT
 WORDS = SPAN * PITCH
@@ -83,7 +84,7 @@
 
 def exchange(x, rows_n, cols_n):
     f32 = jnp.float32
-    any_spec = pl.BlockSpec(memory_space=pl.ANY)
+    any_spec = pl.BlockSpec(memory_space=pltpu.HBM)
     return pl.pallas_call(
         functools.partial(exchange_kernel, rows_n, cols_n),
         out_shape=(
@@ -109,16 +110,20 @@
     )(x)
 
 
-def word(q, r):
-    return (q + FRONT) * PITCH + r + 1
+def cut_of(q, r):
+    if 0 <= r < STRIP:
+        return 0, pl.ds((q + FRONT) * PITCH + r, 8, stride=PITCH)
+    return 1, pl.ds((q + FRONT) * RIM + (r > 0), 8, stride=RIM)
 
 
 def take(ref, q, r):
-    return ref[pl.ds(word(q, r), 8, stride=PITCH), :]
+    which, cut = cut_of(q, r)
+    return ref[which][cut, :]
 
 
 def put(ref, q, r, value):
-    ref[pl.ds(word(q, r), 8, stride=PITCH), :] = value
+    which, cut = cut_of(q, r)
+    ref[which][cut, :] = value
 
 
 def slopes(state, q0, act):
@@ -145,19 +150,25 @@
 
 
 def edges(refs, q0):
-    for ref in refs:
-        put(ref, q0, -1, pltpu.roll(take(ref, q0, STRIP - 1), TILES, 1))
-        put(ref, q0, STRIP, pltpu.roll(take(ref, q0, 0), 128 - TILES, 1))
+    rows = [(ref, pltpu.roll(take(ref, q0, STRIP - 1), TILES, 1), pltpu.roll(take(ref, q0, 0), 128 - TILES, 1)) for ref in refs]
+
+    def store():
+        for ref, low, high in rows:
+            put(ref, q0, -1, low)
+            put(ref, q0, STRIP, high)
+
+    return store
 
 
 def sweep(first, blocks, work, late, unroll):
     trips, rest = divmod(blocks, unroll)
 
     def trip(start, count, before):
+        stores = [late(start + 8 * (k - before)) for k in range(before)]
         for k in range(count):
             work(start + 8 * k)
-        for k in range(before):
-            late(start + 8 * (k - before))
+        for store in stores:
+            store()
 
     trip(first, unroll, 0)
 
@@ -174,17 +185,19 @@
         left = [last + 8 * (k - unroll) for k in range(unroll)]
 
     def finish():
-        for q in left:
-            late(q)
+        for store in [late(q) for q in left]:
+            store()
 
     return finish
 
 
 def window_kernel(x, north, south, sides, corners, out,
-                  grid, turned, side_in, corner_in, pe, pu, pv, pw, qe, qu, qv, qw,
-                  ce, cu, cv, cw, de, du, dv, sems, out_sems):
+                  grid, side_in, corner_in, sems, out_sems, *state):
     level = lax.axis_index("level")
     copies = []
+    fields, rims = list(state[:18]), list(state[18:])
+    pe, pu, pv, qe, qu, qv, ce, cu, cv = zip(fields[:9], rims)
+    pw, qw, cw, de, du, dv, fe, fu, fv = ((one,) for one in fields[9:])
 
     def fetch(src, dst):
         copies.append(pltpu.make_async_copy(src, dst, sems.at[len(copies)]))
@@ -243,8 +256,8 @@
             put(ref, 136, r, beside[8:16])
 
     def weigh(i, carry):
-        at = pl.ds(pl.multiple_of(i * 8 * 11, 8), 8 * 11)
-        pw[at, :] = (pe[at, :] + REST) * pv[at, :]
+        at = pl.ds(pl.multiple_of(i * 8 * PITCH, 8), 8 * PITCH)
+        pw[0][at, :] = (pe[0][at, :] + REST) * pv[0][at, :]
         return carry
 
     lax.fori_loop(0, SPAN // 8, weigh, 0)
@@ -258,8 +271,8 @@
         return e, u, v, (e + REST) * v
 
     a_state, b_state = (pe, pu, pv, pw), (qe, qu, qv, qw)
-    c_state, d_state = (ce, cu, cv, cw), (de, du, dv)
-    nothing = lambda q: None
+    c_state, d_states = (ce, cu, cv, cw), ((de, du, dv), (fe, fu, fv))
+    nothing = lambda q: lambda: None
 
     def predict(now, then, m, with_c):
         def work(q0):
@@ -267,25 +280,23 @@
                 new = tuple(p - g for p, g in zip(own, change))
                 keep(then, q0, r, weighed(new))
                 if with_c and m == 0:
-                    keep(d_state, q0, r, tuple(p - 0.5 * g for p, g in zip(own, change)))
+                    keep(d_states[1], q0, r, tuple(p - 0.5 * g for p, g in zip(own, change)))
                 elif with_c:
-                    mid = tuple(take(ref, q0, r) - 0.5 * g for ref, g in zip(d_state, change))
+                    mid = tuple(take(ref, q0, r) - 0.5 * g for ref, g in zip(d_states[m % 2], change))
                     keep(c_state, q0, r, weighed(mid))
 
             slopes(now, q0, act)
 
         def late(q0):
-            if with_c and m:
-                edges(c_state[:3], q0)
-            edges(then[:3], q0)
+            return edges(c_state[:3] + then[:3] if with_c and m else then[:3], q0)
 
         reach = STEPS - m
-        return sweep(-reach, (128 + 2 * reach + 7) // 8, work, late, 2)
+        return sweep(-reach, (128 + 2 * reach + 7) // 8, work, late, 2 if with_c else 2)
 
     def correct(m):
         def work(q0):
             def act(r, own, change):
-                keep(d_state, q0, r, tuple(take(ref, q0, r) - g for ref, g in zip(d_state, change)))
+                keep(d_states[(m + 1) % 2], q0, r, tuple(take(ref, q0, r) - g for ref, g in zip(d_states[m % 2], change)))
 
             slopes(c_state, q0, act)
 
@@ -295,7 +306,7 @@
     def last():
         def work(q0):
             def act(r, own, change):
-                keep(c_state, q0, r, tuple(take(ref, q0, r) - 0.5 * g for ref, g in zip(d_state, change)))
+                keep(c_state, q0, r, tuple(take(ref, q0, r) - 0.5 * g for ref, g in zip(d_states[0], change)))
 
             slopes(a_state, q0, act)
 
@@ -340,7 +351,7 @@
 
 def window(x, north, south, sides, corners):
     f32 = jnp.float32
-    any_spec = pl.BlockSpec(memory_space=pl.ANY)
+    any_spec = pl.BlockSpec(memory_space=pltpu.HBM)
     return pl.pallas_call(
         window_kernel,
         out_shape=jax.ShapeDtypeStruct((1, 3, ROWS, COLS), f32),
@@ -348,14 +359,12 @@
         out_specs=any_spec,
         scratch_shapes=[
             VMEM((3, 20, 10, 8, 128), f32),
-            VMEM((8, 128), f32),
             VMEM((3, 128, 128), f32),
             VMEM((4, 16, 128), f32),
-        ] + [VMEM((WORDS, 128), f32) for _ in range(15)] + [
             pltpu.SemaphoreType.DMA((3 * TILES + 3,)),
             pltpu.SemaphoreType.DMA((3 * TILES,)),
-        ],
-        compiler_params=pltpu.CompilerParams(vmem_limit_bytes=48 * 1024 * 1024),
+        ] + [VMEM((WORDS, 128), f32) for _ in range(18)] + [VMEM((SPAN * RIM, 128), f32) for _ in range(9)],
+        compiler_params=pltpu.CompilerParams(),
     )(x, north, south, sides, corners)
 
 

time: 44.8 us -> 36.5 us (0.81)
  Pallas kernels: 41.1 us -> 36.3 us
  local copies, waits for them, and re-layouts: 3.41 us -> 0 us
    pallas_call x1, Pallas kernels: 22.8 us -> 18.2 us  [window(): pl.pallas_call(window_kernel, out_shape=jax.ShapeDtypeStruct((1, 3, ROWS,...]
    unnamed x10 -> x0, local copies, waits for them, and re-layouts: 3.41 us -> none
where the time goes in v1:
time: 36.5 us; the launch traced here: 36.3 us
  Pallas kernels  36.3 us (99%)
    pallas_call x1, Pallas kernels, window(): pl.pallas_call(window_kernel, out_shape=jax.ShapeDtypeStruct((1, 3, ROWS,...  18.2 us
    pallas_call x1, Pallas kernels, exchange(): pl.pallas_call(functools.partial(exchange_kernel, rows_n, cols_n), out_sh...  18.1 us

profile of v1, /device:TPU:64, one launch (start us, length us, event | category | flops | bytes accessed | tf_op | source)
XLA Modules:
  0.0 36.3 jit_solution(10651698431046539834)
XLA Ops:
  0.0 18.1 %shard_map.17 = (f32[3,16,1024]{2,1,0:T(8,128)}, f32[3,16,1024]{2,1,0:T(8,128)}, f32[2,3,16,128]{3,2,1,0:T(8,128)}, f32[4,16,128]{2,1,0:T(8,128)}) custom-call(f32[3,128,1024]{2,1,0:T(8,128)} %x.3), custom_call_target="tpu_custom_call" | custom-call | tf_op jit(solution)/shard_map/pallas_call | solution.py:88
  18.1 18.2 %shard_map.18 = f32[1,3,128,1024]{3,2,1,0:T(8,128)} custom-call(f32[3,128,1024]{2,1,0:T(8,128)} %x.3, f32[3,16,1024]{2,1,0:T(8,128)} %get-tuple-element.9.north, f32[3,16,1024]{2,1,0:T(8,128)} %get-tuple-element.10.south, f32[2,3,16,128]{3,2,1,0:T(8,128)} %get-tuple-element.11.sides, f32[4,16,128]{2,1,0:T(8,128)} %get-tuple-element.12.corners), custom_call_target="tpu_custom_call" | custom-call | tf_op jit(solution)/shard_map/pallas_call | solution.py:355

commit v2 on v1

v2 whole, which is shorter than its diff:
```python
import functools

import jax
import jax.numpy as jnp
from jax import lax
from jax.experimental import pallas as pl
from jax.experimental.pallas import tpu as pltpu
from jax.sharding import PartitionSpec as P

STEPS = 8
TIME_STEP = 0.1
GRAVITY = 1.0
ROTATION = 0.2

HALF = 0.5 * TIME_STEP
SCALES = (HALF * HALF * GRAVITY, HALF, HALF)
REST = HALF * HALF * GRAVITY
TURN = TIME_STEP * ROTATION

ROWS = 128
COLS = 1024
TILES = COLS // 128
STRIP = 9
STRIPS = 16
PITCH = 9
RIM = 3
FRONT = 16
SPAN = 128 + 2 * FRONT
WORDS = SPAN * PITCH
VMEM = pltpu.VMEM


def exchange_kernel(rows_n, cols_n, x, north, south, sides, corners,
                    top, bottom, left, right, side_out, corner_out, send, recv):
    me_r, me_c = lax.axis_index("row"), lax.axis_index("col")
    up, down = lax.rem(me_r + rows_n - 1, rows_n), lax.rem(me_r + 1, rows_n)
    west, east = lax.rem(me_c + cols_n - 1, cols_n), lax.rem(me_c + 1, cols_n)
    places = [(up, me_c), (down, me_c), (me_r, west), (me_r, east), (up, west), (up, east), (down, west), (down, east)]
    ids = [{"row": r, "col": c} for r, c in places]
    barrier = pltpu.get_barrier_semaphore()
    for where in ids:
        pl.semaphore_signal(barrier, inc=1, device_id=where, device_id_type=pl.DeviceIdType.MESH)
    lane = lax.broadcasted_iota(jnp.int32, (16, 128), 1)
    view = x.reshape(3, ROWS // 8, 8 * TILES, 128)
    for f in range(3):
        for k, ref in enumerate((left, right)):
            column = (TILES - 1) * k * 8
            ref[f] = view[f, :, column:column + 8, :].reshape(ROWS, 128)
    ends = (left, right)
    for f in range(3):
        side_out[0, 9 * f:9 * f + 9] = jnp.transpose(left[f])[0:9]
        side_out[1, 9 * f:9 * f + 9] = jnp.transpose(right[f])[119:128]
        top[f, 0:64] = x[f, 0:64]
        bottom[f, 0:64] = x[f, 8 * ROWS - 64:8 * ROWS]
        top[f, 64:72] = x[f, pl.ds(64, TILES, stride=8), :]
        bottom[f, 64:72] = x[f, pl.ds(8 * ROWS - 128 + 7, TILES, stride=8), :]
    for k, (ref, row0, lane0) in enumerate(((0, 0, 0), (1, 0, 112), (0, ROWS - 16, 0), (1, ROWS - 16, 112))):
        out = ends[ref][0, row0:row0 + 16]
        if lane0:
            out = pltpu.roll(out, 128 - lane0, 1)
        for f in (1, 2):
            piece = pltpu.roll(ends[ref][f, row0:row0 + 16], (128 - lane0 + 16 * f) % 128, 1)
            out = jnp.where(lane < 16 * f, out, piece)
        corner_out[k] = out
    pl.semaphore_wait(barrier, 8)
    sends = []
    pieces = [
        (top, south), (bottom, north),
        (side_out.at[0], sides.at[0]), (side_out.at[1], sides.at[1]),
        (corner_out.at[0], corners.at[3]), (corner_out.at[1], corners.at[2]),
        (corner_out.at[2], corners.at[1]), (corner_out.at[3], corners.at[0]),
    ]
    for k, (src, dst) in enumerate(pieces):
        sends.append(pltpu.make_async_remote_copy(
            src_ref=src, dst_ref=dst, send_sem=send.at[k], recv_sem=recv.at[k],
            device_id=ids[k], device_id_type=pl.DeviceIdType.MESH))
    for k in (4, 5, 6, 7, 2, 3, 0, 1):
        sends[k].start()
    for one in sends:
        one.wait()


def exchange(x, rows_n, cols_n):
    f32 = jnp.float32
    inside = pl.BlockSpec(memory_space=pltpu.VMEM)
    return pl.pallas_call(
        functools.partial(exchange_kernel, rows_n, cols_n),
        out_shape=(
            jax.ShapeDtypeStruct((3, 72, 128), f32),
            jax.ShapeDtypeStruct((3, 72, 128), f32),
            jax.ShapeDtypeStruct((2, 32, 128), f32),
            jax.ShapeDtypeStruct((4, 16, 128), f32),
        ),
        in_specs=[inside],
        out_specs=(inside,) * 4,
        scratch_shapes=[
            VMEM((3, 72, 128), f32),
            VMEM((3, 72, 128), f32),
            VMEM((3, ROWS, 128), f32),
            VMEM((3, ROWS, 128), f32),
            VMEM((2, 32, 128), f32),
            VMEM((4, 16, 128), f32),
            pltpu.SemaphoreType.DMA((8,)),
            pltpu.SemaphoreType.DMA((8,)),
        ],
        compiler_params=pltpu.CompilerParams(collective_id=0, has_side_effects=True, vmem_limit_bytes=8 * 1024 * 1024),
    )(x)


def cut_of(q, r):
    if 0 <= r < STRIP:
        return 0, pl.ds((q + FRONT) * PITCH + r, 8, stride=PITCH)
    return 1, pl.ds((q + FRONT) * RIM + (r > 0), 8, stride=RIM)


def take(ref, q, r):
    which, cut = cut_of(q, r)
    return ref[which][cut, :]


def put(ref, q, r, value):
    which, cut = cut_of(q, r)
    ref[which][cut, :] = value


def slopes(state, q0, act):
    e_ref, u_ref, v_ref = state

    def load(r):
        e, u, v = take(e_ref, q0, r), take(u_ref, q0, r), take(v_ref, q0, r)
        return e, u, v, (e + REST) * u

    below, here = load(-1), load(0)
    for r in range(STRIP):
        above = load(r + 1)
        e, u, v, _ = here
        de, du, dv, dw = (a - b for a, b in zip(above, below))
        east, west = ((take(e_ref, q, r), take(v_ref, q, r)) for q in (q0 + 1, q0 - 1))
        ye, yv = east[0] - west[0], east[1] - west[1]
        yu = take(u_ref, q0 + 1, r) - take(u_ref, q0 - 1, r)
        ge = dw + ((east[0] + REST) * east[1] - (west[0] + REST) * west[1])
        gu = (u * du + v * (yu - TURN)) + de
        gv = (u * (dv + TURN) + v * yv) + ye
        act(r, (e, u, v), (ge, gu, gv))
        below, here = here, above


def edges(refs, q0):
    rows = [(ref, pltpu.roll(take(ref, q0, STRIP - 1), TILES, 1), pltpu.roll(take(ref, q0, 0), 128 - TILES, 1)) for ref in refs]

    def store():
        for ref, low, high in rows:
            put(ref, q0, -1, low)
            put(ref, q0, STRIP, high)

    return store


def sweep(first, blocks, work, late, unroll):
    trips, rest = divmod(blocks, unroll)

    def trip(start, count, before):
        stores = [late(start + 8 * (k - before)) for k in range(before)]
        for k in range(count):
            work(start + 8 * k)
        for store in stores:
            store()

    trip(first, unroll, 0)

    def step(i, carry):
        trip(first + 8 * unroll * i, unroll, unroll)
        return carry

    lax.fori_loop(1, trips, step, 0)
    last = first + 8 * unroll * trips
    if rest:
        trip(last, rest, unroll)
        left = [last + 8 * k for k in range(rest)]
    else:
        left = [last + 8 * (k - unroll) for k in range(unroll)]

    def finish():
        for store in [late(q) for q in left]:
            store()

    return finish


def window_kernel(x, north, south, sides, corners, out, turned, beside, final, out_sems, *state):
    level = lax.axis_index("level")
    fields, rims = list(state[:15]), list(state[15:])
    pe, pu, pv, qe, qu, qv, ce, cu, cv = zip(fields[:9], rims)
    de, du, dv, fe, fu, fv = ((one,) for one in fields[9:])

    lane = lax.broadcasted_iota(jnp.int32, (16, 128), 1)
    for f in range(3):
        turned[f, 0:9] = sides[0, 9 * f:9 * f + 9]
        turned[f, 119:128] = sides[1, 9 * f:9 * f + 9]
        beside[f, 16:144] = jnp.transpose(turned[f])
        for k, place in ((0, 0), (2, 144)):
            west, east = pltpu.roll(corners[k], 112 - 16 * f, 1), corners[k + 1]
            if f:
                east = pltpu.roll(east, 128 - 16 * f, 1)
            beside[f, place:place + 16] = jnp.where(lane < 64, east, west)

    def tile_row(f, i):
        if i == -9:
            return north[f, 64:72]
        if i == ROWS + 8:
            return south[f, 64:72]
        if i < 0:
            return north[f, pl.ds(i + 8, TILES, stride=8), :]
        if i >= ROWS:
            return south[f, pl.ds(i - ROWS, TILES, stride=8), :]
        return x[f, pl.ds((i // 8) * 64 + i % 8, TILES, stride=8), :]

    strip_of = lax.broadcasted_iota(jnp.int32, (8, 128), 1) % TILES
    for f, ref in enumerate((pe, pu, pv)):
        outer = []
        for start in (-1, 7):
            block = [beside[f, pl.ds(16 + STRIP * s - 8 + start, 8), :] for s in range(STRIPS)]
            outer.append(jnp.transpose(jnp.concatenate(block, axis=0)) * SCALES[f])
        for r in range(-1, STRIP + 1):
            here = jnp.concatenate([tile_row(f, s * STRIP + r - 8) for s in range(STRIPS)], axis=0)
            here = jnp.transpose(here) * SCALES[f]
            for k in range(16):
                put(ref, 8 * k, r, here[8 * k:8 * k + 8])
            at = r + 1
            far = outer[at // 8]
            at %= 8
            for q in (-16, -8, 128, 136):
                k = q % 128
                toward, mine = (1, 0) if q < 0 else (127, TILES - 1)
                inner = pltpu.roll(here[k:k + 8], toward, 1)
                given = far[k:k + 8]
                if mine != at:
                    given = pltpu.roll(given, (mine - at) % 128, 1)
                put(ref, q, r, jnp.where(strip_of == mine, given, inner))

    def keep(refs, q, r, values):
        for ref, value in zip(refs, values):
            put(ref, q, r, value)

    a_state, b_state = (pe, pu, pv), (qe, qu, qv)
    c_state, d_states = (ce, cu, cv), ((de, du, dv), (fe, fu, fv))
    nothing = lambda q: lambda: None

    def predict(now, then, m, with_c):
        def work(q0):
            def act(r, own, change):
                new = tuple(p - g for p, g in zip(own, change))
                keep(then, q0, r, new)
                if with_c and m == 0:
                    keep(d_states[1], q0, r, tuple(p - 0.5 * g for p, g in zip(own, change)))
                elif with_c:
                    mid = tuple(take(ref, q0, r) - 0.5 * g for ref, g in zip(d_states[m % 2], change))
                    keep(c_state, q0, r, mid)

            slopes(now, q0, act)

        def late(q0):
            return edges(c_state + then if with_c and m else then, q0)

        reach = STEPS - m
        return sweep(-reach, (128 + 2 * reach + 7) // 8, work, late, 2)

    def correct(m):
        def work(q0):
            def act(r, own, change):
                keep(d_states[(m + 1) % 2], q0, r, tuple(take(ref, q0, r) - g for ref, g in zip(d_states[m % 2], change)))

            slopes(c_state, q0, act)

        reach = STEPS - 1 - m
        return sweep(-reach, (128 + 2 * reach + 7) // 8, work, nothing, 2)

    def last():
        def work(q0):
            def act(r, own, change):
                keep(c_state, q0, r, tuple(take(ref, q0, r) - 0.5 * g for ref, g in zip(d_states[0], change)))

            slopes(a_state, q0, act)

        sweep(0, 16, work, nothing, 2)

    def emit(refs):
        done = []
        for f, ref in enumerate(refs):
            for r in range(STRIP):
                block = jnp.concatenate([take(ref, 8 * k, r) for k in range(16)], axis=0)
                block = jnp.transpose(block) * (1.0 / SCALES[f])
                for s in range(STRIPS):
                    i = s * STRIP + r - 8
                    if 0 <= i < ROWS:
                        final[f, pl.ds((i // 8) * 64 + i % 8, TILES, stride=8), :] = block[8 * s:8 * s + 8]
            done.append(pltpu.make_async_copy(final.at[f], out.at[0, f], out_sems.at[f]))
            done[-1].start()
        for copy in done:
            copy.wait()

    @pl.when(level == 0)
    def _():
        for m in range(STEPS):
            now, then = (a_state, b_state) if m % 2 == 0 else (b_state, a_state)
            predict(now, then, m, False)()
        emit(a_state)

    @pl.when(level == 1)
    def _():
        for m in range(STEPS):
            now, then = (a_state, b_state) if m % 2 == 0 else (b_state, a_state)
            predict(now, then, m, True)()
            if m:
                correct(m)
        last()
        emit(c_state)


def window(x, *halo):
    f32 = jnp.float32
    inside = pl.BlockSpec(memory_space=pltpu.VMEM)
    return pl.pallas_call(
        window_kernel,
        out_shape=jax.ShapeDtypeStruct((1, 3, ROWS * TILES, 128), f32),
        in_specs=[inside] * 5,
        out_specs=pl.BlockSpec(memory_space=pltpu.HBM),
        scratch_shapes=[
            VMEM((3, 128, 128), f32),
            VMEM((3, 160, 128), f32),
            VMEM((3, ROWS * TILES, 128), f32),
            pltpu.SemaphoreType.DMA((3,)),
        ] + [VMEM((WORDS, 128), f32) for _ in range(15)] + [VMEM((SPAN * RIM, 128), f32) for _ in range(9)],
        compiler_params=pltpu.CompilerParams(vmem_limit_bytes=32 * 1024 * 1024),
    )(x, *halo)


def solution(mesh):
    rows_n, cols_n = mesh.shape["row"], mesh.shape["col"]

    def body(x):
        words = x.reshape(3, ROWS // 8, 8, TILES, 128).transpose(0, 1, 3, 2, 4).reshape(3, ROWS * TILES, 128)
        done = window(words, *exchange(words, rows_n, cols_n))
        return done.reshape(1, 3, ROWS // 8, TILES, 8, 128).transpose(0, 1, 2, 4, 3, 5).reshape(1, 3, ROWS, COLS)

    return jax.shard_map(
        body,
        mesh=mesh,
        in_specs=(P(None, "row", "col"),),
        out_specs=P("level", None, "row", "col"),
        check_vma=False,
    )
```

time: 36.5 us -> 33.6 us (0.921)
  Pallas kernels: 36.3 us -> 32 us
  local copies, waits for them, and re-layouts: 0 us -> 1.41 us
    pallas_call x1, Pallas kernels: 18.2 us -> 14.8 us  [window(): pl.pallas_call(window_kernel, out_shape=jax.ShapeDtypeStruct((1, 3, ROWS...]
    unnamed x0 -> x4, local copies, waits for them, and re-layouts: none -> 1.41 us
    pallas_call x1, Pallas kernels: 18.1 us -> 17.2 us  [exchange(): pl.pallas_call(functools.partial(exchange_kernel, rows_n, cols_n), out_sh...]
where the time goes in v2:
time: 33.6 us; the launch traced here: 33.4 us
  Pallas kernels  32 us (95%)
  local copies, waits for them, and re-layouts  1.41 us (4%)
    pallas_call x1, Pallas kernels, exchange(): pl.pallas_call(functools.partial(exchange_kernel, rows_n, cols_n), out_sh...  17.2 us
    pallas_call x1, Pallas kernels, window(): pl.pallas_call(window_kernel, out_shape=jax.ShapeDtypeStruct((1, 3, ROWS...  14.8 us
    unnamed x4, local copies, waits for them, and re-layouts  1.41 us

profile of v2, /device:TPU:64, one launch (start us, length us, event | category | flops | bytes accessed | tf_op | source)
XLA Modules:
  0.0 33.4 jit_solution(11654677929064534373)
XLA Ops:
  0.0 0.0 copy-start
  0.0 1.4 %copy-done = f32[3,128,1024]{2,1,0:T(8,128)S(1)} copy-done((f32[3,128,1024]{2,1,0:T(8,128)S(1)}, f32[3,128,1024]{2,1,0:T(8,128)}, u32[]{:S(2)}) %copy-start) | copy-done | bytes 1572888
  1.4 0.0 copy-start.1
  1.4 17.2 %shard_map.17 = (f32[3,72,128]{2,1,0:T(8,128)S(1)}, f32[3,72,128]{2,1,0:T(8,128)S(1)}, f32[2,32,128]{2,1,0:T(8,128)S(1)}, f32[4,16,128]{2,1,0:T(8,128)S(1)}) custom-call(f32[3,1024,128]{2,1,0:T(8,128)S(1)} %bitcast.10), custom_call_target="tpu_custom_call" | custom-call | tf_op jit(solution)/shard_map/pallas_call | solution.py:86
  18.6 0.0 copy-done.1
  18.6 14.8 %shard_map.18 = f32[1,3,1024,128]{3,2,1,0:T(8,128)} custom-call(f32[3,1024,128]{2,1,0:T(8,128)S(1)} %bitcast.11, f32[3,72,128]{2,1,0:T(8,128)S(1)} %get-tuple-element.9.north, f32[3,72,128]{2,1,0:T(8,128)S(1)} %get-tuple-element.10.south, f32[2,32,128]{2,1,0:T(8,128)S(1)} %get-tuple-element.11.sides, f32[4,16,128]{2,1,0:T(8,128)S(1)} %get-tuple-element.12.corners), custom_call_target="tpu_custom_call" | custom-call | tf_op jit(solution)/shard_map/pallas_call | solution.py:323
Async XLA Ops:
  0.0 1.4 %copy-start = (f32[3,128,1024]{2,1,0:T(8,128)S(1)}, f32[3,128,1024]{2,1,0:T(8,128)}, u32[]{:S(2)}) copy-start(f32[3,128,1024]{2,1,0:T(8,128)} %param.1) | copy-start | bytes 4718596
  1.4 17.2 %copy-start.1 = (f32[3,128,1024]{2,1,0:T(8,128)S(1)}, f32[3,128,1024]{2,1,0:T(8,128)}, u32[]{:S(2)}) copy-start(f32[3,128,1024]{2,1,0:T(8,128)} %param.1) | copy-start | bytes 4718596

commit v3 on v2

v3 whole, which is shorter than its diff:
```python
import functools

import jax
import jax.numpy as jnp
from jax import lax
from jax.experimental import pallas as pl
from jax.experimental.pallas import tpu as pltpu
from jax.sharding import PartitionSpec as P

STEPS = 8
TIME_STEP = 0.1
GRAVITY = 1.0
ROTATION = 0.2

HALF = 0.5 * TIME_STEP
SCALES = (HALF * HALF * GRAVITY, HALF, HALF)
REST = HALF * HALF * GRAVITY
TURN = TIME_STEP * ROTATION

ROWS = 128
COLS = 1024
TILES = COLS // 128
STRIP = 9
STRIPS = 16
PITCH = 9
RIM = 3
FRONT = 16
SPAN = 128 + 2 * FRONT
WORDS = SPAN * PITCH
VMEM = pltpu.VMEM


def meet(places):
    barrier = pltpu.get_barrier_semaphore()
    for where in places:
        pl.semaphore_signal(barrier, inc=1, device_id=where, device_id_type=pl.DeviceIdType.MESH)
    return barrier


def remote(k, src, dst, where, send, recv):
    return pltpu.make_async_remote_copy(
        src_ref=src, dst_ref=dst, send_sem=send.at[k], recv_sem=recv.at[k],
        device_id=where, device_id_type=pl.DeviceIdType.MESH)


def around(axis, count):
    me = lax.axis_index(axis)
    return lax.rem(me + count - 1, count), lax.rem(me + 1, count)


def rows_kernel(rows_n, x, north, south, top, bottom, send, recv):
    up, down = around("row", rows_n)
    barrier = meet([{"row": up}, {"row": down}])
    for f in range(3):
        top[f, 0:64] = x[f, 0:64]
        bottom[f, 0:64] = x[f, 8 * ROWS - 64:8 * ROWS]
        top[f, 64:72] = x[f, pl.ds(64, TILES, stride=8), :]
        bottom[f, 64:72] = x[f, pl.ds(8 * ROWS - 128 + 7, TILES, stride=8), :]
        top[f, 72:80] = jnp.zeros((8, 128), jnp.float32)
        bottom[f, 72:80] = jnp.zeros((8, 128), jnp.float32)
    pl.semaphore_wait(barrier, 2)
    copies = [remote(0, top, south, {"row": up}, send, recv), remote(1, bottom, north, {"row": down}, send, recv)]
    for copy in copies:
        copy.start()
    for copy in copies:
        copy.wait()


def swap_rows(x, rows_n):
    f32 = jnp.float32
    inside = pl.BlockSpec(memory_space=pltpu.VMEM)
    return pl.pallas_call(
        functools.partial(rows_kernel, rows_n),
        out_shape=(jax.ShapeDtypeStruct((3, 80, 128), f32), jax.ShapeDtypeStruct((3, 80, 128), f32)),
        in_specs=[inside],
        out_specs=(inside,) * 2,
        scratch_shapes=[
            VMEM((3, 80, 128), f32),
            VMEM((3, 80, 128), f32),
            pltpu.SemaphoreType.DMA((2,)),
            pltpu.SemaphoreType.DMA((2,)),
        ],
        compiler_params=pltpu.CompilerParams(collective_id=0, has_side_effects=True, vmem_limit_bytes=4 * 1024 * 1024),
    )(x)


def cut_of(q, r):
    if 0 <= r < STRIP:
        return 0, pl.ds((q + FRONT) * PITCH + r, 8, stride=PITCH)
    return 1, pl.ds((q + FRONT) * RIM + (r > 0), 8, stride=RIM)


def take(ref, q, r):
    which, cut = cut_of(q, r)
    return ref[which][cut, :]


def put(ref, q, r, value):
    which, cut = cut_of(q, r)
    ref[which][cut, :] = value


def slopes(state, q0, act):
    e_ref, u_ref, v_ref = state

    def load(r):
        e, u, v = take(e_ref, q0, r), take(u_ref, q0, r), take(v_ref, q0, r)
        return e, u, v, (e + REST) * u

    below, here = load(-1), load(0)
    for r in range(STRIP):
        above = load(r + 1)
        e, u, v, _ = here
        de, du, dv, dw = (a - b for a, b in zip(above, below))
        east, west = ((take(e_ref, q, r), take(v_ref, q, r)) for q in (q0 + 1, q0 - 1))
        ye, yv = east[0] - west[0], east[1] - west[1]
        yu = take(u_ref, q0 + 1, r) - take(u_ref, q0 - 1, r)
        ge = dw + ((east[0] + REST) * east[1] - (west[0] + REST) * west[1])
        gu = (u * du + v * (yu - TURN)) + de
        gv = (u * (dv + TURN) + v * yv) + ye
        act(r, (e, u, v), (ge, gu, gv))
        below, here = here, above


def edges(refs, q0):
    rows = [(ref, pltpu.roll(take(ref, q0, STRIP - 1), TILES, 1), pltpu.roll(take(ref, q0, 0), 128 - TILES, 1)) for ref in refs]

    def store():
        for ref, low, high in rows:
            put(ref, q0, -1, low)
            put(ref, q0, STRIP, high)

    return store


def sweep(first, blocks, work, late, unroll):
    trips, rest = divmod(blocks, unroll)

    def trip(start, count, before):
        stores = [late(start + 8 * (k - before)) for k in range(before)]
        for k in range(count):
            work(start + 8 * k)
        for store in stores:
            store()

    trip(first, unroll, 0)

    def step(i, carry):
        trip(first + 8 * unroll * i, unroll, unroll)
        return carry

    lax.fori_loop(1, trips, step, 0)
    last = first + 8 * unroll * trips
    if rest:
        trip(last, rest, unroll)
        left = [last + 8 * k for k in range(rest)]
    else:
        left = [last + 8 * (k - unroll) for k in range(unroll)]

    def finish():
        for store in [late(q) for q in left]:
            store()

    return finish


def run(level, a_state, b_state, c_state, d_states, out_state, origin, width, early=None):
    nothing = lambda q: lambda: None

    def keep(refs, q, r, values):
        for ref, value in zip(refs, values):
            put(ref, q, r, value)

    def blocks(reach):
        return origin - reach, (width + 2 * reach + 7) // 8

    def predict(now, then, m, with_c):
        def work(q0):
            def act(r, own, change):
                keep(then, q0, r, tuple(p - g for p, g in zip(own, change)))
                if with_c and m == 0:
                    keep(d_states[1], q0, r, tuple(p - 0.5 * g for p, g in zip(own, change)))
                elif with_c:
                    keep(c_state, q0, r, tuple(take(ref, q0, r) - 0.5 * g for ref, g in zip(d_states[m % 2], change)))

            slopes(now, q0, act)

        def late(q0):
            return edges(c_state + then if with_c and m else then, q0)

        end = m == STEPS - 1 and not with_c
        return sweep(*blocks(STEPS - m), work, nothing if end else late, 2)

    def correct(m):
        def work(q0):
            def act(r, own, change):
                keep(d_states[(m + 1) % 2], q0, r, tuple(take(ref, q0, r) - g for ref, g in zip(d_states[m % 2], change)))

            slopes(c_state, q0, act)

        return sweep(*blocks(STEPS - 1 - m), work, nothing, 2)

    def last():
        def work(q0):
            def act(r, own, change):
                keep(out_state, q0, r, tuple(take(ref, q0, r) - 0.5 * g for ref, g in zip(d_states[0], change)))

            slopes(a_state, q0, act)

        sweep(*blocks(0), work, nothing, 2)

    def steps(with_c):
        for m in range(STEPS):
            if early is not None:
                early(with_c, m)
            now, then = (a_state, b_state) if m % 2 == 0 else (b_state, a_state)
            if m == STEPS - 1 and not with_c:
                then = out_state
            predict(now, then, m, with_c)()
            if with_c and m:
                correct(m)
        if with_c:
            last()
        if early is not None:
            early(with_c, STEPS)

    @pl.when(level == 0)
    def _():
        steps(False)

    @pl.when(level == 1)
    def _():
        steps(True)


def split_state(state):
    fields, rims = list(state[:15]), list(state[15:])
    pairs = list(zip(fields[:9], rims))
    single = [(one,) for one in fields[9:]]
    return tuple(pairs[:3]), tuple(pairs[3:6]), tuple(pairs[6:9]), (tuple(single[:3]), tuple(single[3:6]))


def state_scratch(span):
    f32 = jnp.float32
    return [VMEM((span * PITCH, 128), f32) for _ in range(15)] + [VMEM((span * RIM, 128), f32) for _ in range(9)]


SEND_AHEAD = ((STEPS, 4, 2, 0), (5, 2, 1, 0))


def main_kernel(rows_n, cols_n, x, north, south, sides, corners, oe, ou, ov,
                side_out, corner_out, send, recv, *state):
    level = lax.axis_index("level")
    up, down = around("row", rows_n)
    west, east = around("col", cols_n)
    ids = [{"col": west}, {"col": east}] + [{"row": r, "col": c} for r in (up, down) for c in (west, east)]
    barrier = meet(ids)
    group = lax.rem(lax.axis_index("col"), len(SEND_AHEAD[0]))

    lane = lax.broadcasted_iota(jnp.int32, (16, 128), 1)
    view = x.reshape(3, ROWS // 8, 8 * TILES, 128)

    def column(f, c, t0, t1):
        return view[f, t0:t1, 8 * c:8 * c + 8, :].reshape(8 * (t1 - t0), 128)

    for f in range(3):
        side_out[0, 9 * f:9 * f + 9] = jnp.transpose(column(f, 0, 0, 16))[0:9]
        side_out[1, 9 * f:9 * f + 9] = jnp.transpose(column(f, TILES - 1, 0, 16))[119:128]
    for k, (c, t, lane0) in enumerate(((0, 0, 0), (TILES - 1, 0, 112), (0, 14, 0), (TILES - 1, 14, 112))):
        out = column(0, c, t, t + 2)
        if lane0:
            out = pltpu.roll(out, 128 - lane0, 1)
        for f in (1, 2):
            piece = pltpu.roll(column(f, c, t, t + 2), (128 - lane0 + 16 * f) % 128, 1)
            out = jnp.where(lane < 16 * f, out, piece)
        corner_out[k] = out
    pieces = [(side_out.at[0], sides.at[0]), (side_out.at[1], sides.at[1])]
    pieces += [(corner_out.at[k], corners.at[3 - k]) for k in range(4)]
    copies = [remote(k, *piece, where, send, recv) for k, (piece, where) in enumerate(zip(pieces, ids))]

    def early(with_c, m):
        turns = SEND_AHEAD[int(with_c)]
        for k, turn in enumerate(turns):
            if turn == m:
                @pl.when(group == k)
                def _():
                    pl.semaphore_wait(barrier, 6)
                    for copy in copies:
                        copy.start()

    a_state, b_state, c_state, d_states = split_state(state)

    def tile_row(f, i):
        if i == -9:
            return north[f, 64:72]
        if i == ROWS + 8:
            return south[f, 64:72]
        if i < 0:
            return north[f, pl.ds(i + 8, TILES, stride=8), :]
        if i >= ROWS:
            return south[f, pl.ds(i - ROWS, TILES, stride=8), :]
        return x[f, pl.ds((i // 8) * 64 + i % 8, TILES, stride=8), :]

    for f, ref in enumerate(a_state):
        for r in range(-1, STRIP + 1):
            here = jnp.concatenate([tile_row(f, s * STRIP + r - 8) for s in range(STRIPS)], axis=0)
            here = jnp.transpose(here) * SCALES[f]
            for k in range(16):
                put(ref, 8 * k, r, here[8 * k:8 * k + 8])
            for q in (-16, -8, 128, 136):
                k = q % 128
                put(ref, q, r, pltpu.roll(here[k:k + 8], 1 if q < 0 else 127, 1))

    run(level, a_state, b_state, c_state, d_states, ((oe,), (ou,), (ov,)), 0, 128, early)
    for copy in copies:
        copy.wait()


def main(x, north, south, rows_n, cols_n):
    f32 = jnp.float32
    inside = pl.BlockSpec(memory_space=pltpu.VMEM)
    return pl.pallas_call(
        functools.partial(main_kernel, rows_n, cols_n),
        out_shape=(
            jax.ShapeDtypeStruct((2, 32, 128), f32),
            jax.ShapeDtypeStruct((4, 16, 128), f32),
        ) + (jax.ShapeDtypeStruct((WORDS, 128), f32),) * 3,
        in_specs=[inside] * 3,
        out_specs=(inside,) * 5,
        scratch_shapes=[
            VMEM((2, 32, 128), f32),
            VMEM((4, 16, 128), f32),
            pltpu.SemaphoreType.DMA((6,)),
            pltpu.SemaphoreType.DMA((6,)),
        ] + state_scratch(SPAN),
        compiler_params=pltpu.CompilerParams(collective_id=1, has_side_effects=True, vmem_limit_bytes=32 * 1024 * 1024),
    )(x, north, south)


BAND = 9
BAND_SPAN = 64


def band_kernel(x, north, south, sides, corners, oe, ou, ov, out, turned, beside, band, final, out_sems, be, bu, bv, *state):
    level = lax.axis_index("level")
    a_state, b_state, c_state, d_states = split_state(state)
    lane16 = lax.broadcasted_iota(jnp.int32, (16, 128), 1)
    lane8 = lax.broadcasted_iota(jnp.int32, (8, 128), 1)

    for f in range(3):
        turned[f, 0:9] = sides[0, 9 * f:9 * f + 9]
        turned[f, 119:128] = sides[1, 9 * f:9 * f + 9]
        beside[f, 16:144] = jnp.transpose(turned[f])
        for k, place in ((0, 0), (2, 144)):
            west, east = pltpu.roll(corners[k], 112 - 16 * f, 1), corners[k + 1]
            if f:
                east = pltpu.roll(east, 128 - 16 * f, 1)
            beside[f, place:place + 16] = jnp.where(lane16 < 64, east, west)

    def own(f, c, t):
        if t == -2:
            return north[f, 57 + c:65 + c]
        if t == -1:
            return north[f, 8 * c:8 * c + 8]
        if t == 16:
            return south[f, 8 * c:8 * c + 8]
        if t == 17:
            return south[f, 64 + c:72 + c]
        return x[f, 64 * t + 8 * c:64 * t + 8 * c + 8]

    for f in range(3):
        for t in range(-2, 18):
            row = 8 * (t + 2)
            outer = beside[f, row:row + 8]
            low = pltpu.roll(jnp.where(lane8 >= 64, outer, own(f, 0, t)), 9, 1)
            high = pltpu.roll(jnp.where(lane8 < 64, outer, own(f, TILES - 1, t)), 82, 1)
            band[f, row:row + 8] = jnp.where(lane8 < 64, low, high)

    strip_of = lane8 % TILES
    for f, ref in enumerate(a_state):
        blocks = []
        for start in (-1, 7):
            block = [band[f, pl.ds(16 + STRIP * s - 8 + start, 8), :] for s in range(STRIPS)]
            blocks.append(jnp.transpose(jnp.concatenate(block, axis=0)) * SCALES[f])
        for r in range(-1, STRIP + 1):
            far, at = blocks[(r + 1) // 8], (r + 1) % 8
            for k in range(4):
                low, high = far[8 * k:8 * k + 8], far[64 + 8 * k:72 + 8 * k]
                if at:
                    low = pltpu.roll(low, 128 - at, 1)
                if at != TILES - 1:
                    high = pltpu.roll(high, TILES - 1 - at, 1)
                put(ref, 8 * k, r, jnp.where(strip_of == TILES - 1, high, low))

    b_out = ((be,), (bu,), (bv,))
    run(level, a_state, b_state, c_state, d_states, b_out, BAND, BAND)

    word_of = lax.broadcasted_iota(jnp.int32, (8, 128), 0)
    first, end = strip_of == 0, strip_of == TILES - 1
    done = []
    for f, (ref, fix) in enumerate(zip((oe, ou, ov), b_out)):
        for r in range(STRIP):
            block = [take((ref,), 8 * k, r) for k in range(16)]
            block[0] = jnp.where(first, take(fix, 9, r), block[0])
            block[1] = jnp.where(first & (word_of == 0), take(fix, 17, r), block[1])
            block[14] = jnp.where(end & (word_of == 7), take(fix, 2, r), block[14])
            block[15] = jnp.where(end, take(fix, 10, r), block[15])
            block = jnp.transpose(jnp.concatenate(block, axis=0)) * (1.0 / SCALES[f])
            for s in range(STRIPS):
                i = s * STRIP + r - 8
                if 0 <= i < ROWS:
                    final[f, pl.ds((i // 8) * 64 + i % 8, TILES, stride=8), :] = block[8 * s:8 * s + 8]
        done.append(pltpu.make_async_copy(final.at[f], out.at[0, f], out_sems.at[f]))
        done[-1].start()
    for copy in done:
        copy.wait()


def bands(x, *rest):
    f32 = jnp.float32
    inside = pl.BlockSpec(memory_space=pltpu.VMEM)
    return pl.pallas_call(
        band_kernel,
        out_shape=jax.ShapeDtypeStruct((1, 3, ROWS * TILES, 128), f32),
        in_specs=[inside] * 8,
        out_specs=pl.BlockSpec(memory_space=pltpu.HBM),
        scratch_shapes=[
            VMEM((3, 128, 128), f32),
            VMEM((3, 160, 128), f32),
            VMEM((3, 160, 128), f32),
            VMEM((3, ROWS * TILES, 128), f32),
            pltpu.SemaphoreType.DMA((3,)),
        ] + [VMEM((BAND_SPAN * PITCH, 128), f32) for _ in range(3)] + state_scratch(BAND_SPAN),
        compiler_params=pltpu.CompilerParams(vmem_limit_bytes=16 * 1024 * 1024),
    )(x, *rest)


def solution(mesh):
    rows_n, cols_n = mesh.shape["row"], mesh.shape["col"]

    def body(x):
        words = x.reshape(3, ROWS // 8, 8, TILES, 128).transpose(0, 1, 3, 2, 4).reshape(3, ROWS * TILES, 128)
        north, south = swap_rows(words, rows_n)
        done = bands(words, north, south, *main(words, north, south, rows_n, cols_n))
        return done.reshape(1, 3, ROWS // 8, TILES, 8, 128).transpose(0, 1, 2, 4, 3, 5).reshape(1, 3, ROWS, COLS)

    return jax.shard_map(
        body,
        mesh=mesh,
        in_specs=(P(None, "row", "col"),),
        out_specs=P("level", None, "row", "col"),
        check_vma=False,
    )
```

time: 33.6 us -> 31.3 us (0.932)
  the two profiles are of different devices: /device:TPU:64 before, /device:TPU:89 now
where the time goes in v3:
time: 31.3 us; the launch traced here: 31.2 us
  Pallas kernels  29.8 us (95%)
  local copies, waits for them, and re-layouts  1.41 us (5%)
    pallas_call x1, Pallas kernels, main(): pl.pallas_call(functools.partial(main_kernel, rows_n, cols_n), out_shape=...  18.7 us
    pallas_call x1, Pallas kernels, swap_rows(): pl.pallas_call(functools.partial(rows_kernel, rows_n), out_shape=(jax.Sha...  6.54 us
    pallas_call x1, Pallas kernels, bands(): pl.pallas_call(band_kernel, out_shape=jax.ShapeDtypeStruct((1, 3, ROWS *...  4.53 us
    unnamed x4, local copies, waits for them, and re-layouts  1.41 us

profile of v3, /device:TPU:89, one launch (start us, length us, event | category | flops | bytes accessed | tf_op | source)
XLA Modules:
  0.0 31.2 jit_solution(14096258479526308928)
XLA Ops:
  0.0 0.0 copy-start
  0.0 1.4 %copy-done = f32[3,128,1024]{2,1,0:T(8,128)S(1)} copy-done((f32[3,128,1024]{2,1,0:T(8,128)S(1)}, f32[3,128,1024]{2,1,0:T(8,128)}, u32[]{:S(2)}) %copy-start) | copy-done | bytes 1572888
  1.4 0.0 copy-start.1
  1.4 6.5 %shard_map.17 = (f32[3,80,128]{2,1,0:T(8,128)S(1)}, f32[3,80,128]{2,1,0:T(8,128)S(1)}) custom-call(f32[3,1024,128]{2,1,0:T(8,128)S(1)} %bitcast.10), custom_call_target="tpu_custom_call" | custom-call | tf_op jit(solution)/shard_map/pallas_call | solution.py:72
  8.0 0.0 copy-done.1
  8.0 18.7 %shard_map.18 = (f32[2,32,128]{2,1,0:T(8,128)S(1)}, f32[4,16,128]{2,1,0:T(8,128)S(1)}, f32[1440,128]{1,0:T(8,128)S(1)}, f32[1440,128]{1,0:T(8,128)S(1)}, f32[1440,128]{1,0:T(8,128)S(1)}) custom-call(f32[3,1024,128]{2,1,0:T(8,128)S(1)} %bitcast.11, f32[3,80,128]{2,1,0:T(8,128)S(1)} %get-tuple-element.12.north, f32[3,80,128]{2,1,0:T(8,128)S(1)} %get-tuple-element.13.south), custom_call_target="tpu_custom_call" | custom-call | tf_op jit(solution)/shard_map/pallas_call | solution.py:322
  26.7 4.5 %shard_map.19 = f32[1,3,1024,128]{3,2,1,0:T(8,128)} custom-call(f32[3,1024,128]{2,1,0:T(8,128)S(1)} %bitcast.12, f32[3,80,128]{2,1,0:T(8,128)S(1)} %get-tuple-element.12.north, f32[3,80,128]{2,1,0:T(8,128)S(1)} %get-tuple-element.13.south, f32[2,32,128]{2,1,0:T(8,128)S(1)} %get-tuple-element.14.sides, f32[4,16,128]{2,1,0:T(8,128)S(1)} %get-tuple-element.15.corners, ...), custom_call_target="tpu_custom_call" | custom-call | tf_op jit(solution)/shard_map/pallas_call | solution.py:422
Async XLA Ops:
  0.0 1.4 %copy-start = (f32[3,128,1024]{2,1,0:T(8,128)S(1)}, f32[3,128,1024]{2,1,0:T(8,128)}, u32[]{:S(2)}) copy-start(f32[3,128,1024]{2,1,0:T(8,128)} %param.1) | copy-start | bytes 4718596
  1.4 6.6 %copy-start.1 = (f32[3,128,1024]{2,1,0:T(8,128)S(1)}, f32[3,128,1024]{2,1,0:T(8,128)}, u32[]{:S(2)}) copy-start(f32[3,128,1024]{2,1,0:T(8,128)} %param.1) | copy-start | bytes 4718596

commit v4 on v3

--- a/solution.py
+++ b/solution.py
@@ -245,38 +245,43 @@
     return [VMEM((span * PITCH, 128), f32) for _ in range(15)] + [VMEM((span * RIM, 128), f32) for _ in range(9)]
 
 
-SEND_AHEAD = ((STEPS, 4, 2, 0), (5, 2, 1, 0))
-
-
-def main_kernel(rows_n, cols_n, x, north, south, sides, corners, oe, ou, ov,
-                side_out, corner_out, send, recv, *state):
+SEND_AHEAD = ((STEPS, 3, 3, 0), (5, 2, 2, 0))
+
+
+def own_tile(x, north, south, f, c, t):
+    if t == -2:
+        return north[f, 57 + c:65 + c]
+    if t == -1:
+        return north[f, 8 * c:8 * c + 8]
+    if t == ROWS // 8:
+        return south[f, 8 * c:8 * c + 8]
+    if t == ROWS // 8 + 1:
+        return south[f, 64 + c:72 + c]
+    return x[f, 64 * t + 8 * c:64 * t + 8 * c + 8]
+
+
+def main_kernel(cols_n, x, north, south, sides, oe, ou, ov, side_out, send, recv, *state):
     level = lax.axis_index("level")
-    up, down = around("row", rows_n)
     west, east = around("col", cols_n)
-    ids = [{"col": west}, {"col": east}] + [{"row": r, "col": c} for r in (up, down) for c in (west, east)]
+    ids = [{"col": west}, {"col": east}]
     barrier = meet(ids)
     group = lax.rem(lax.axis_index("col"), len(SEND_AHEAD[0]))
 
-    lane = lax.broadcasted_iota(jnp.int32, (16, 128), 1)
+    lane = lax.broadcasted_iota(jnp.int32, (8, 128), 1)
     view = x.reshape(3, ROWS // 8, 8 * TILES, 128)
-
-    def column(f, c, t0, t1):
-        return view[f, t0:t1, 8 * c:8 * c + 8, :].reshape(8 * (t1 - t0), 128)
-
-    for f in range(3):
-        side_out[0, 9 * f:9 * f + 9] = jnp.transpose(column(f, 0, 0, 16))[0:9]
-        side_out[1, 9 * f:9 * f + 9] = jnp.transpose(column(f, TILES - 1, 0, 16))[119:128]
-    for k, (c, t, lane0) in enumerate(((0, 0, 0), (TILES - 1, 0, 112), (0, 14, 0), (TILES - 1, 14, 112))):
-        out = column(0, c, t, t + 2)
-        if lane0:
-            out = pltpu.roll(out, 128 - lane0, 1)
-        for f in (1, 2):
-            piece = pltpu.roll(column(f, c, t, t + 2), (128 - lane0 + 16 * f) % 128, 1)
-            out = jnp.where(lane < 16 * f, out, piece)
-        corner_out[k] = out
-    pieces = [(side_out.at[0], sides.at[0]), (side_out.at[1], sides.at[1])]
-    pieces += [(corner_out.at[k], corners.at[3 - k]) for k in range(4)]
-    copies = [remote(k, *piece, where, send, recv) for k, (piece, where) in enumerate(zip(pieces, ids))]
+    for k, (c, lane0) in enumerate(((0, 0), (TILES - 1, 112))):
+        for f in range(3):
+            whole = jnp.transpose(view[f, :, 8 * c:8 * c + 8, :].reshape(ROWS, 128))
+            side_out[k, 9 * f:9 * f + 9] = whole[119:128] if k else whole[0:9]
+        for j, t in enumerate((-2, -1, 16, 17)):
+            out = own_tile(x, north, south, 0, c, t)
+            if lane0:
+                out = pltpu.roll(out, 128 - lane0, 1)
+            for f in (1, 2):
+                piece = pltpu.roll(own_tile(x, north, south, f, c, t), (128 - lane0 + 16 * f) % 128, 1)
+                out = jnp.where(lane < 16 * f, out, piece)
+            side_out[k, 32 + 8 * j:40 + 8 * j] = out
+    copies = [remote(k, side_out.at[k], sides.at[k], ids[k], send, recv) for k in range(2)]
 
     def early(with_c, m):
         turns = SEND_AHEAD[int(with_c)]
@@ -284,7 +289,7 @@
             if turn == m:
                 @pl.when(group == k)
                 def _():
-                    pl.semaphore_wait(barrier, 6)
+                    pl.semaphore_wait(barrier, 2)
                     for copy in copies:
                         copy.start()
 
@@ -316,22 +321,18 @@
         copy.wait()
 
 
-def main(x, north, south, rows_n, cols_n):
+def main(x, north, south, cols_n):
     f32 = jnp.float32
     inside = pl.BlockSpec(memory_space=pltpu.VMEM)
     return pl.pallas_call(
-        functools.partial(main_kernel, rows_n, cols_n),
-        out_shape=(
-            jax.ShapeDtypeStruct((2, 32, 128), f32),
-            jax.ShapeDtypeStruct((4, 16, 128), f32),
-        ) + (jax.ShapeDtypeStruct((WORDS, 128), f32),) * 3,
+        functools.partial(main_kernel, cols_n),
+        out_shape=(jax.ShapeDtypeStruct((2, 64, 128), f32),) + (jax.ShapeDtypeStruct((WORDS, 128), f32),) * 3,
         in_specs=[inside] * 3,
-        out_specs=(inside,) * 5,
+        out_specs=(inside,) * 4,
         scratch_shapes=[
-            VMEM((2, 32, 128), f32),
-            VMEM((4, 16, 128), f32),
-            pltpu.SemaphoreType.DMA((6,)),
-            pltpu.SemaphoreType.DMA((6,)),
+            VMEM((2, 64, 128), f32),
+            pltpu.SemaphoreType.DMA((2,)),
+            pltpu.SemaphoreType.DMA((2,)),
         ] + state_scratch(SPAN),
         compiler_params=pltpu.CompilerParams(collective_id=1, has_side_effects=True, vmem_limit_bytes=32 * 1024 * 1024),
     )(x, north, south)
@@ -341,7 +342,7 @@
 BAND_SPAN = 64
 
 
-def band_kernel(x, north, south, sides, corners, oe, ou, ov, out, turned, beside, band, final, out_sems, be, bu, bv, *state):
+def band_kernel(x, north, south, sides, oe, ou, ov, out, turned, beside, band, final, out_sems, be, bu, bv, *state):
     level = lax.axis_index("level")
     a_state, b_state, c_state, d_states = split_state(state)
     lane16 = lax.broadcasted_iota(jnp.int32, (16, 128), 1)
@@ -351,29 +352,18 @@
         turned[f, 0:9] = sides[0, 9 * f:9 * f + 9]
         turned[f, 119:128] = sides[1, 9 * f:9 * f + 9]
         beside[f, 16:144] = jnp.transpose(turned[f])
-        for k, place in ((0, 0), (2, 144)):
-            west, east = pltpu.roll(corners[k], 112 - 16 * f, 1), corners[k + 1]
+        for k, place in ((32, 0), (48, 144)):
+            west, east = pltpu.roll(sides[1, k:k + 16], 112 - 16 * f, 1), sides[0, k:k + 16]
             if f:
                 east = pltpu.roll(east, 128 - 16 * f, 1)
             beside[f, place:place + 16] = jnp.where(lane16 < 64, east, west)
-
-    def own(f, c, t):
-        if t == -2:
-            return north[f, 57 + c:65 + c]
-        if t == -1:
-            return north[f, 8 * c:8 * c + 8]
-        if t == 16:
-            return south[f, 8 * c:8 * c + 8]
-        if t == 17:
-            return south[f, 64 + c:72 + c]
-        return x[f, 64 * t + 8 * c:64 * t + 8 * c + 8]
 
     for f in range(3):
         for t in range(-2, 18):
             row = 8 * (t + 2)
             outer = beside[f, row:row + 8]
-            low = pltpu.roll(jnp.where(lane8 >= 64, outer, own(f, 0, t)), 9, 1)
-            high = pltpu.roll(jnp.where(lane8 < 64, outer, own(f, TILES - 1, t)), 82, 1)
+            low = pltpu.roll(jnp.where(lane8 >= 64, outer, own_tile(x, north, south, f, 0, t)), 9, 1)
+            high = pltpu.roll(jnp.where(lane8 < 64, outer, own_tile(x, north, south, f, TILES - 1, t)), 82, 1)
             band[f, row:row + 8] = jnp.where(lane8 < 64, low, high)
 
     strip_of = lane8 % TILES
@@ -422,7 +412,7 @@
     return pl.pallas_call(
         band_kernel,
         out_shape=jax.ShapeDtypeStruct((1, 3, ROWS * TILES, 128), f32),
-        in_specs=[inside] * 8,
+        in_specs=[inside] * 7,
         out_specs=pl.BlockSpec(memory_space=pltpu.HBM),
         scratch_shapes=[
             VMEM((3, 128, 128), f32),
@@ -441,7 +431,7 @@
     def body(x):
         words = x.reshape(3, ROWS // 8, 8, TILES, 128).transpose(0, 1, 3, 2, 4).reshape(3, ROWS * TILES, 128)
         north, south = swap_rows(words, rows_n)
-        done = bands(words, north, south, *main(words, north, south, rows_n, cols_n))
+        done = bands(words, north, south, *main(words, north, south, cols_n))
         return done.reshape(1, 3, ROWS // 8, TILES, 8, 128).transpose(0, 1, 2, 4, 3, 5).reshape(1, 3, ROWS, COLS)
 
     return jax.shard_map(

time: 31.3 us -> 29.4 us (0.939)
  the two profiles are of different devices: /device:TPU:89 before, /device:TPU:64 now
where the time goes in v4:
time: 29.4 us; the launch traced here: 29.2 us
  Pallas kernels  27.8 us (95%)
  local copies, waits for them, and re-layouts  1.41 us (5%)
    pallas_call x1, Pallas kernels, main(): pl.pallas_call(functools.partial(main_kernel, cols_n), out_shape=(jax.Sha...  16.2 us
    pallas_call x1, Pallas kernels, swap_rows(): pl.pallas_call(functools.partial(rows_kernel, rows_n), out_shape=(jax.Sha...  7.02 us
    pallas_call x1, Pallas kernels, bands(): pl.pallas_call(band_kernel, out_shape=jax.ShapeDtypeStruct((1, 3, ROWS *...  4.53 us
    unnamed x4, local copies, waits for them, and re-layouts  1.41 us

profile of v4, /device:TPU:64, one launch (start us, length us, event | category | flops | bytes accessed | tf_op | source)
XLA Modules:
  0.0 29.2 jit_solution(6458688526774452136)
XLA Ops:
  0.0 0.0 copy-start
  0.0 1.4 %copy-done = f32[3,128,1024]{2,1,0:T(8,128)S(1)} copy-done((f32[3,128,1024]{2,1,0:T(8,128)S(1)}, f32[3,128,1024]{2,1,0:T(8,128)}, u32[]{:S(2)}) %copy-start) | copy-done | bytes 1572888
  1.4 0.0 copy-start.1
  1.4 7.0 %shard_map.17 = (f32[3,80,128]{2,1,0:T(8,128)S(1)}, f32[3,80,128]{2,1,0:T(8,128)S(1)}) custom-call(f32[3,1024,128]{2,1,0:T(8,128)S(1)} %bitcast.10), custom_call_target="tpu_custom_call" | custom-call | tf_op jit(solution)/shard_map/pallas_call | solution.py:72
  8.4 0.0 copy-done.1
  8.5 16.2 %shard_map.18 = (f32[2,64,128]{2,1,0:T(8,128)S(1)}, f32[1440,128]{1,0:T(8,128)S(1)}, f32[1440,128]{1,0:T(8,128)S(1)}, f32[1440,128]{1,0:T(8,128)S(1)}) custom-call(f32[3,1024,128]{2,1,0:T(8,128)S(1)} %bitcast.11, f32[3,80,128]{2,1,0:T(8,128)S(1)} %get-tuple-element.11.north, f32[3,80,128]{2,1,0:T(8,128)S(1)} %get-tuple-element.12.south), custom_call_target="tpu_custom_call" | custom-call | tf_op jit(solution)/shard_map/pallas_call | solution.py:327
  24.7 4.5 %shard_map.19 = f32[1,3,1024,128]{3,2,1,0:T(8,128)} custom-call(f32[3,1024,128]{2,1,0:T(8,128)S(1)} %bitcast.12, f32[3,80,128]{2,1,0:T(8,128)S(1)} %get-tuple-element.11.north, f32[3,80,128]{2,1,0:T(8,128)S(1)} %get-tuple-element.12.south, f32[2,64,128]{2,1,0:T(8,128)S(1)} %get-tuple-element.13.sides, f32[1440,128]{1,0:T(8,128)S(1)} %get-tuple-element.14.oe, ...), custom_call_target="tpu_custom_call" | custom-call | tf_op jit(solution)/shard_map/pallas_call | solution.py:412
Async XLA Ops:
  0.0 1.4 %copy-start = (f32[3,128,1024]{2,1,0:T(8,128)S(1)}, f32[3,128,1024]{2,1,0:T(8,128)}, u32[]{:S(2)}) copy-start(f32[3,128,1024]{2,1,0:T(8,128)} %param.1) | copy-start | bytes 4718596
  1.4 7.0 %copy-start.1 = (f32[3,128,1024]{2,1,0:T(8,128)S(1)}, f32[3,128,1024]{2,1,0:T(8,128)}, u32[]{:S(2)}) copy-start(f32[3,128,1024]{2,1,0:T(8,128)} %param.1) | copy-start | bytes 4718596

commit v5 on v4

--- a/solution.py
+++ b/solution.py
@@ -133,17 +133,17 @@
     return store
 
 
-def sweep(first, blocks, work, late, unroll):
+def sweep(first, blocks, work, late, unroll, opening=None):
     trips, rest = divmod(blocks, unroll)
 
-    def trip(start, count, before):
-        stores = [late(start + 8 * (k - before)) for k in range(before)]
+    def trip(start, count, before, opening=None):
+        stores = opening() if opening else [late(start + 8 * (k - before)) for k in range(before)]
         for k in range(count):
             work(start + 8 * k)
         for store in stores:
             store()
 
-    trip(first, unroll, 0)
+    trip(first, unroll, 0, opening)
 
     def step(i, carry):
         trip(first + 8 * unroll * i, unroll, unroll)
@@ -157,11 +157,7 @@
     else:
         left = [last + 8 * (k - unroll) for k in range(unroll)]
 
-    def finish():
-        for store in [late(q) for q in left]:
-            store()
-
-    return finish
+    return lambda: [late(q) for q in left]
 
 
 def run(level, a_state, b_state, c_state, d_states, out_state, origin, width, early=None):
@@ -191,14 +187,14 @@
         end = m == STEPS - 1 and not with_c
         return sweep(*blocks(STEPS - m), work, nothing if end else late, 2)
 
-    def correct(m):
+    def correct(m, opening):
         def work(q0):
             def act(r, own, change):
                 keep(d_states[(m + 1) % 2], q0, r, tuple(take(ref, q0, r) - g for ref, g in zip(d_states[m % 2], change)))
 
             slopes(c_state, q0, act)
 
-        return sweep(*blocks(STEPS - 1 - m), work, nothing, 2)
+        sweep(*blocks(STEPS - 1 - m), work, nothing, 2, opening)
 
     def last():
         def work(q0):
@@ -216,9 +212,13 @@
             now, then = (a_state, b_state) if m % 2 == 0 else (b_state, a_state)
             if m == STEPS - 1 and not with_c:
                 then = out_state
-            predict(now, then, m, with_c)()
+            rest = predict(now, then, m, with_c)
+            far = width > 64
+            if not (far and with_c and m):
+                for store in rest():
+                    store()
             if with_c and m:
-                correct(m)
+                correct(m, rest if far else None)
         if with_c:
             last()
         if early is not None:
@@ -245,7 +245,7 @@
     return [VMEM((span * PITCH, 128), f32) for _ in range(15)] + [VMEM((span * RIM, 128), f32) for _ in range(9)]
 
 
-SEND_AHEAD = ((STEPS, 3, 3, 0), (5, 2, 2, 0))
+SEND_AHEAD = ((STEPS, 5, 5, 0), (7, 3, 3, 0))
 
 
 def own_tile(x, north, south, f, c, t):

time: 29.4 us -> 27.4 us (0.932)
  Pallas kernels: 27.8 us -> 25.8 us
    pallas_call x1, Pallas kernels: 16.2 us -> 14.2 us  [main(): pl.pallas_call(functools.partial(main_kernel, cols_n), out_shape=(jax.Sha...]
where the time goes in v5:
time: 27.4 us; the launch traced here: 27.2 us
  Pallas kernels  25.8 us (94%)
  local copies, waits for them, and re-layouts  1.41 us (5%)
    pallas_call x1, Pallas kernels, main(): pl.pallas_call(functools.partial(main_kernel, cols_n), out_shape=(jax.Sha...  14.2 us
    pallas_call x1, Pallas kernels, swap_rows(): pl.pallas_call(functools.partial(rows_kernel, rows_n), out_shape=(jax.Sha...  7.02 us
    pallas_call x1, Pallas kernels, bands(): pl.pallas_call(band_kernel, out_shape=jax.ShapeDtypeStruct((1, 3, ROWS *...  4.53 us
    unnamed x4, local copies, waits for them, and re-layouts  1.41 us

profile of v5, /device:TPU:64, one launch (start us, length us, event | category | flops | bytes accessed | tf_op | source)
XLA Modules:
  0.0 27.2 jit_solution(14571850776746101466)
XLA Ops:
  0.0 0.0 copy-start
  0.0 1.4 %copy-done = f32[3,128,1024]{2,1,0:T(8,128)S(1)} copy-done((f32[3,128,1024]{2,1,0:T(8,128)S(1)}, f32[3,128,1024]{2,1,0:T(8,128)}, u32[]{:S(2)}) %copy-start) | copy-done | bytes 1572888
  1.4 0.0 copy-start.1
  1.4 7.0 %shard_map.17 = (f32[3,80,128]{2,1,0:T(8,128)S(1)}, f32[3,80,128]{2,1,0:T(8,128)S(1)}) custom-call(f32[3,1024,128]{2,1,0:T(8,128)S(1)} %bitcast.10), custom_call_target="tpu_custom_call" | custom-call | tf_op jit(solution)/shard_map/pallas_call | solution.py:72
  8.4 0.0 copy-done.1
  8.5 14.2 %shard_map.18 = (f32[2,64,128]{2,1,0:T(8,128)S(1)}, f32[1440,128]{1,0:T(8,128)S(1)}, f32[1440,128]{1,0:T(8,128)S(1)}, f32[1440,128]{1,0:T(8,128)S(1)}) custom-call(f32[3,1024,128]{2,1,0:T(8,128)S(1)} %bitcast.11, f32[3,80,128]{2,1,0:T(8,128)S(1)} %get-tuple-element.11.north, f32[3,80,128]{2,1,0:T(8,128)S(1)} %get-tuple-element.12.south), custom_call_target="tpu_custom_call" | custom-call | tf_op jit(solution)/shard_map/pallas_call | solution.py:327
  22.7 4.5 %shard_map.19 = f32[1,3,1024,128]{3,2,1,0:T(8,128)} custom-call(f32[3,1024,128]{2,1,0:T(8,128)S(1)} %bitcast.12, f32[3,80,128]{2,1,0:T(8,128)S(1)} %get-tuple-element.11.north, f32[3,80,128]{2,1,0:T(8,128)S(1)} %get-tuple-element.12.south, f32[2,64,128]{2,1,0:T(8,128)S(1)} %get-tuple-element.13.sides, f32[1440,128]{1,0:T(8,128)S(1)} %get-tuple-element.14.oe, ...), custom_call_target="tpu_custom_call" | custom-call | tf_op jit(solution)/shard_map/pallas_call | solution.py:412
Async XLA Ops:
  0.0 1.4 %copy-start = (f32[3,128,1024]{2,1,0:T(8,128)S(1)}, f32[3,128,1024]{2,1,0:T(8,128)}, u32[]{:S(2)}) copy-start(f32[3,128,1024]{2,1,0:T(8,128)} %param.1) | copy-start | bytes 4718596
  1.4 7.0 %copy-start.1 = (f32[3,128,1024]{2,1,0:T(8,128)S(1)}, f32[3,128,1024]{2,1,0:T(8,128)}, u32[]{:S(2)}) copy-start(f32[3,128,1024]{2,1,0:T(8,128)} %param.1) | copy-start | bytes 4718596
